TPU v7x, 32 devices: a whole 2x2x4 slice. The times are simulated.
32 devices in a mesh: dp: 4 (over y, x), seq: 8 (over z, core).
Axes of the slice: x: 2, y: 2, z: 4, core: 2. Of those that a mesh axis runs over, the one named last changes fastest.
Arguments:
- queries: bfloat16 [4, 2048, 16, 128], P('dp', 'seq'), may hold values from -9 to 9
- keys: bfloat16 [4, 2048, 8, 128], P('dp', 'seq'), may hold values from -9 to 9
- values: bfloat16 [4, 2048, 8, 128], P('dp', 'seq'), may hold values from -6 to 6
- doc_lengths: int32 [4, 8], P('dp'), may hold values from 1 to 1536, 2048 in all within a row
Outputs:
- attended: bfloat16 [4, 2048, 16, 128], P('dp', 'seq')
- z_loss: float32 [], replicated
Inputs may be any that keep to these rules, and one draw needn't show every extreme that they name: `doc_lengths`: each row's 8 lengths add up to 2048, and its longest document has exactly 1536 tokens.
All inputs are finite; a program needn't handle non-finite values.
Results may differ from a plain program's by a relative error of at most 0.012.
Values may be sent and summed in bfloat16 or wider, within the bound.
A program may use at most 64 MiB of HBM per device.

v0:
```python
import jax
import jax.numpy as jnp
from jax import lax
from jax.sharding import PartitionSpec as P

WINDOW = 1024


rope_base = 500000.0
score_scale = 1.0 / 12.0
masked = -1e30


def shifted(block, axis, distance):
    devices = range(lax.axis_size(axis))
    route = [(i - distance, i) for i in devices if i - distance in devices]
    return lax.ppermute(block, axis, route)


def rotate(tensor, places):
    half = tensor.shape[-1] // 2
    frequency = rope_base ** (-2.0 * jnp.arange(half, dtype=jnp.float32) / tensor.shape[-1])
    angles = places.astype(jnp.float32)[..., None, None] * frequency
    cos_table = jnp.cos(angles)
    sin_table = jnp.sin(angles)
    widened = tensor.astype(jnp.float32)
    front_half = widened[..., :half]
    back_half = widened[..., half:]
    joined = jnp.concatenate(
        [
            front_half * cos_table - back_half * sin_table,
            back_half * cos_table + front_half * sin_table,
        ],
        axis=-1,
    )
    return joined.astype(jnp.bfloat16)


def doc_index(doc_ends, where_at):
    return jnp.sum((doc_ends[None, :] <= where_at[:, None]).astype(jnp.int32), axis=1)


def shards(queries, keys, values, doc_lengths):
    block_rows = queries.shape[1]
    query_heads = queries.shape[2]
    head_width = queries.shape[3]
    key_heads = keys.shape[2]
    group_size = query_heads // key_heads
    seq_shards = lax.axis_size("seq")
    seq_index = lax.axis_index("seq")
    reach_blocks = min(WINDOW // block_rows, seq_shards - 1)
    doc_sizes = doc_lengths[0]
    doc_ends = jnp.cumsum(doc_sizes)
    doc_starts = doc_ends - doc_sizes
    own_rows = seq_index * block_rows + jnp.arange(block_rows, dtype=jnp.int32)
    own_doc = doc_index(doc_ends, own_rows)
    chosen = own_doc[:, None] == jnp.arange(doc_sizes.shape[0], dtype=jnp.int32)[None, :]
    own_start = jnp.sum(jnp.where(chosen, doc_starts[None, :], 0), axis=1)
    query_rot = rotate(queries[0], own_rows - own_start)
    key_rot = jnp.transpose(rotate(keys[0], own_rows - own_start), (1, 0, 2))
    value_own = jnp.transpose(values[0], (1, 0, 2))
    grouped = jnp.transpose(
        query_rot.reshape(block_rows, key_heads, group_size, head_width), (1, 0, 2, 3)
    )
    key_list = [key_rot]
    value_list = [value_own]
    current = (key_rot, value_own)
    for hop_index in range(reach_blocks):
        current = shifted((current[0], current[1]), "seq", 1)
        key_list.append(current[0])
        value_list.append(current[1])
    near_keys = jnp.concatenate(key_list, axis=1)
    near_values = jnp.concatenate(value_list, axis=1)
    per_step = max(1, 512 // block_rows)
    step_count = -(-(reach_blocks + 1) // per_step)
    step_rows = per_step * block_rows
    extra_rows = step_count * step_rows - near_keys.shape[1]
    padded_keys = jnp.pad(near_keys, ((0, 0), (0, extra_rows), (0, 0)))
    padded_values = jnp.pad(near_values, ((0, 0), (0, extra_rows), (0, 0)))
    stack_rows = jnp.arange(step_count * step_rows, dtype=jnp.int32)
    key_at = (seq_index - stack_rows // block_rows) * block_rows + stack_rows % block_rows
    key_doc = doc_index(doc_ends, key_at)
    visible_all = (
        (own_doc[:, None] == key_doc[None, :])
        & (key_at[None, :] <= own_rows[:, None])
        & (own_rows[:, None] - key_at[None, :] < WINDOW)
        & (key_at[None, :] >= 0)
    )

    def visit(step_index, carry):
        begin = step_index * step_rows
        keys_step = lax.dynamic_slice_in_dim(padded_keys, begin, step_rows, 1)
        values_step = lax.dynamic_slice_in_dim(padded_values, begin, step_rows, 1)
        visible_step = lax.dynamic_slice_in_dim(visible_all, begin, step_rows, 1)

        def update(state):
            old_peak, old_total, old_summed = state
            scores = (
                jnp.einsum("ktgd,kud->kgtu", grouped, keys_step, preferred_element_type=jnp.float32)
                * score_scale
            )
            scores = jnp.where(visible_step[None, None], scores, masked)
            new_peak = jnp.maximum(old_peak, jnp.max(scores, axis=-1))
            weights = jnp.where(
                visible_step[None, None], jnp.exp(scores - new_peak[..., None]), 0.0
            )
            rescale = jnp.exp(old_peak - new_peak)
            new_total = old_total * rescale + jnp.sum(weights, axis=-1)
            product = jnp.einsum(
                "kgtu,kud->kgtd",
                weights.astype(jnp.bfloat16),
                values_step,
                preferred_element_type=jnp.float32,
            )
            return (new_peak, new_total, old_summed * rescale[..., None] + product)

        def unchanged(state):
            return state

        return lax.cond(jnp.any(visible_step), update, unchanged, carry)

    start_peak = jnp.full((key_heads, group_size, block_rows), masked, jnp.float32)
    start_total = jnp.zeros((key_heads, group_size, block_rows), jnp.float32)
    start_summed = jnp.zeros((key_heads, group_size, block_rows, head_width), jnp.float32)
    peak, total, summed = lax.fori_loop(
        0, step_count, visit, (start_peak, start_total, start_summed)
    )
    mixed = summed / total[..., None]
    normalizers = peak + jnp.log(total)
    attended = (
        jnp.transpose(mixed, (2, 0, 1, 3))
        .reshape(block_rows, query_heads, head_width)
        .astype(jnp.bfloat16)
    )
    local_squares = jnp.sum(normalizers * normalizers)
    all_squares = lax.psum(local_squares, ("dp", "seq"))
    z_loss = all_squares / (lax.axis_size("dp") * seq_shards * block_rows * query_heads)
    return (attended[None], z_loss)


def solution(mesh):
    placed = (
        P("dp", "seq", None, None),
        P("dp", "seq", None, None),
        P("dp", "seq", None, None),
        P("dp", None),
    )
    return jax.shard_map(
        shards,
        mesh=mesh,
        in_specs=placed,
        out_specs=(P("dp", "seq", None, None), P()),
        check_vma=False,
    )
```

profile of v0, /device:TPU:16, one launch (start us, length us, event | category | flops | bytes accessed | tf_op | source)
XLA Modules:
  0.0 138.3 jit_solution(14540733339655485135)
XLA Ops:
  5.6 1.9 %collective-permute-start = (bf16[8,256,128]{2,1,0:T(8,128)(2,1)S(1)}, bf16[8,256,128]{2,1,0:T(8,128)(2,1)S(1)}, u32[]{:S(2)}, u32[]{:S(2)}) collective-permute-start(bf16[8,256,128]{2,1,0:T(8,128)(2,1)S(1)} %get-tuple-element.247), channel_id=1, source_target_pairs={{0,1},{1,2},{2,3},{3,4},{4,5},{5,6},{6,7},{8,9},{9,10},{10,11},{11... | collective-permute-start | bytes 1572872 | tf_op jit(solution)/shard_map/ppermute | solution.py:17
  7.6 3.6 %collective-permute-start.4 = (bf16[8,256,128]{2,1,0:T(8,128)(2,1)S(1)}, bf16[8,256,128]{2,1,0:T(8,128)(2,1)S(1)}, u32[]{:S(2)}, u32[]{:S(2)}) collective-permute-start(bf16[8,256,128]{2,1,0:T(8,128)(2,1)S(1)} %bitcast.71), channel_id=1, source_target_pairs={{0,1},{1,2},{2,3},{3,4},{4,5},{5,6},{6,7},{8,9},{9,10},{10,11},{11... | collective-permute-start | bytes 1572872 | tf_op jit(solution)/shard_map/ppermute | solution.py:17
  11.4 4.8 %collective-permute-done = bf16[8,256,128]{2,1,0:T(8,128)(2,1)S(1)} collective-permute-done((bf16[8,256,128]{2,1,0:T(8,128)(2,1)S(1)}, bf16[8,256,128]{2,1,0:T(8,128)(2,1)S(1)}, u32[]{:S(2)}, u32[]{:S(2)}) %collective-permute-start) | collective-permute-done | bytes 524320 | tf_op jit(solution)/shard_map/ppermute | solution.py:17
  16.1 1.9 %collective-permute-start.1 = (bf16[8,256,128]{2,1,0:T(8,128)(2,1)S(1)}, bf16[8,256,128]{2,1,0:T(8,128)(2,1)S(1)}, u32[]{:S(2)}, u32[]{:S(2)}) collective-permute-start(bf16[8,256,128]{2,1,0:T(8,128)(2,1)S(1)} %collective-permute-done), channel_id=1, source_target_pairs={{0,1},{1,2},{2,3},{3,4},{4,5},{5,6},{6,7},{8,9},{9,10},{10,11},{11... | collective-permute-start | bytes 1572872 | tf_op jit(solution)/shard_map/ppermute | solution.py:17
  18.0 2.4 %fusion.19 = pred[256,1536]{0,1:T(8,128)(4,1)} fusion(s32[256]{0:T(256)S(1)} %iota_add_fusion, s32[256]{0:T(256)S(1)} %convert_reduce_fusion.1, s32[1536]{0:T(1024)S(1)} %fusion.29, s32[1536]{0:T(1024)S(1)} %convert_reduce_fusion, pred[1536]{0:T(1024)(128)(4,1)S(1)} %broadcast_compare_fusion), kind=kLoop, calls=%fused_computation.26 | loop fusion | flops 2752512 | bytes 409088 | tf_op jit(solution)/shard_map/and | solution.py:84
  21.7 2.2 %collective-permute-start.5 = (bf16[8,256,128]{2,1,0:T(8,128)(2,1)S(1)}, bf16[8,256,128]{2,1,0:T(8,128)(2,1)}, u32[]{:S(2)}, u32[]{:S(2)}) collective-permute-start(bf16[8,256,128]{2,1,0:T(8,128)(2,1)S(1)} %collective-permute-done.4), channel_id=1, source_target_pairs={{0,1},{1,2},{2,3},{3,4},{4,5},{5,6},{6,7},{8,9},{9,10},{10,11},{11... | collective-permute-start | bytes 1572872 | tf_op jit(solution)/shard_map/ppermute | solution.py:17
  24.2 3.2 %collective-permute-done.1 = bf16[8,256,128]{2,1,0:T(8,128)(2,1)S(1)} collective-permute-done((bf16[8,256,128]{2,1,0:T(8,128)(2,1)S(1)}, bf16[8,256,128]{2,1,0:T(8,128)(2,1)S(1)}, u32[]{:S(2)}, u32[]{:S(2)}) %collective-permute-start.1) | collective-permute-done | bytes 524320 | tf_op jit(solution)/shard_map/ppermute | solution.py:17
  27.4 1.9 %collective-permute-start.2 = (bf16[8,256,128]{2,1,0:T(8,128)(2,1)S(1)}, bf16[8,256,128]{2,1,0:T(8,128)(2,1)}, u32[]{:S(2)}, u32[]{:S(2)}) collective-permute-start(bf16[8,256,128]{2,1,0:T(8,128)(2,1)S(1)} %collective-permute-done.1), channel_id=1, source_target_pairs={{0,1},{1,2},{2,3},{3,4},{4,5},{5,6},{6,7},{8,9},{9,10},{10,11},{11... | collective-permute-start | bytes 1572872 | tf_op jit(solution)/shard_map/ppermute | solution.py:17
  30.6 2.5 %collective-permute-done.5 = bf16[8,256,128]{2,1,0:T(8,128)(2,1)} collective-permute-done((bf16[8,256,128]{2,1,0:T(8,128)(2,1)S(1)}, bf16[8,256,128]{2,1,0:T(8,128)(2,1)}, u32[]{:S(2)}, u32[]{:S(2)}) %collective-permute-start.5) | collective-permute-done | bytes 524320 | tf_op jit(solution)/shard_map/ppermute | solution.py:17
  33.1 1.9 %collective-permute-start.6 = (bf16[8,256,128]{2,1,0:T(8,128)(2,1)}, bf16[8,256,128]{2,1,0:T(8,128)(2,1)}, u32[]{:S(2)}, u32[]{:S(2)}) collective-permute-start(bf16[8,256,128]{2,1,0:T(8,128)(2,1)} %collective-permute-done.5), channel_id=1, source_target_pairs={{0,1},{1,2},{2,3},{3,4},{4,5},{5,6},{6,7},{8,9},{9,10},{10,11},{11... | collective-permute-start | bytes 1572872 | tf_op jit(solution)/shard_map/ppermute | solution.py:17
  36.5 2.2 %collective-permute-done.2 = bf16[8,256,128]{2,1,0:T(8,128)(2,1)} collective-permute-done((bf16[8,256,128]{2,1,0:T(8,128)(2,1)S(1)}, bf16[8,256,128]{2,1,0:T(8,128)(2,1)}, u32[]{:S(2)}, u32[]{:S(2)}) %collective-permute-start.2) | collective-permute-done | bytes 524320 | tf_op jit(solution)/shard_map/ppermute | solution.py:17
  38.7 1.9 %collective-permute-start.3 = (bf16[8,256,128]{2,1,0:T(8,128)(2,1)}, bf16[8,256,128]{2,1,0:T(8,128)(2,1)S(1)}, u32[]{:S(2)}, u32[]{:S(2)}) collective-permute-start(bf16[8,256,128]{2,1,0:T(8,128)(2,1)} %collective-permute-done.2), channel_id=1, source_target_pairs={{0,1},{1,2},{2,3},{3,4},{4,5},{5,6},{6,7},{8,9},{9,10},{10,11},{11... | collective-permute-start | bytes 1572872 | tf_op jit(solution)/shard_map/ppermute | solution.py:17
  40.7 3.6 %collective-permute-done.6 = bf16[8,256,128]{2,1,0:T(8,128)(2,1)} collective-permute-done((bf16[8,256,128]{2,1,0:T(8,128)(2,1)}, bf16[8,256,128]{2,1,0:T(8,128)(2,1)}, u32[]{:S(2)}, u32[]{:S(2)}) %collective-permute-start.6) | collective-permute-done | bytes 524320 | tf_op jit(solution)/shard_map/ppermute | solution.py:17
  44.3 1.9 %collective-permute-start.7 = (bf16[8,256,128]{2,1,0:T(8,128)(2,1)}, bf16[8,256,128]{2,1,0:T(8,128)(2,1)S(1)}, u32[]{:S(2)}, u32[]{:S(2)}) collective-permute-start(bf16[8,256,128]{2,1,0:T(8,128)(2,1)} %collective-permute-done.6), channel_id=1, source_target_pairs={{0,1},{1,2},{2,3},{3,4},{4,5},{5,6},{6,7},{8,9},{9,10},{10,11},{11... | collective-permute-start | bytes 1572872 | tf_op jit(solution)/shard_map/ppermute | solution.py:17
  48.2 2.0 %constant_dynamic-update-slice_fusion.1 = bf16[8,1280,128]{2,1,0:T(8,128)(2,1)} fusion(bf16[8,1280,128]{2,1,0:T(8,128)(2,1)} %constant_dynamic-update-slice_fusion.2, bf16[8,256,128]{2,1,0:T(8,128)(2,1)} %collective-permute-done.2), kind=kLoop, calls=%fused_computation.39 | loop fusion | bytes 1048576
  52.2 3.7 %pad.7 = bf16[8,1536,128]{2,1,0:T(8,128)(2,1)} pad(bf16[8,1280,128]{2,1,0:T(8,128)(2,1)} %constant_dynamic-update-slice_fusion, bf16[]{:T(256)} %constant.118.clone.1), padding=0_0x0_256x0_0 | pad | bytes 5767170 | tf_op jit(solution)/shard_map/jit(_pad)/pad | solution.py:78
  56.0 2.0 %pad.8 = bf16[8,1536,128]{2,1,0:T(8,128)(2,1)} pad(bf16[8,1280,128]{2,1,0:T(8,128)(2,1)S(1)} %constant_dynamic-update-slice_fusion.5, bf16[]{:T(256)} %constant.118.clone.1), padding=0_0x0_256x0_0 | pad | bytes 5767170 | tf_op jit(solution)/shard_map/jit(_pad)/pad | solution.py:79
  58.2 34.5 %while.17 = (s32[]{:T(128)}, f32[8,2,256]{2,1,0:T(2,128)S(1)}, f32[8,2,256]{2,1,0:T(2,128)S(1)}, f32[8,2,256,128]{3,2,1,0:T(8,128)S(1)}, pred[256,1536]{0,1:T(8,...) while((s32[]{:T(128)}, f32[8,2,256]{2,1,0:T(2,128)S(1)}, ...), condition=%wide.region_10.11_spmd, body=%wide.region_4.10_spmd.sunk | while | flops 1102192640 | bytes 33424676 | solution.py:125
  60.6 9.1 %conditional.2 = ((f32[8,2,256]{2,1,0:T(2,128)S(1)}, f32[8,2,256]{2,1,0:T(2,128)S(1)}, f32[8,2,256,128]{3,2,1,0:T(8,128)S(1)})) conditional(s32[]{:T(128)} %convert_element_type.83, (f32[8,2,256]{2,1,0:T(2,128)S(1)}, f32[8,2,256]{2,1,0:T(2,128)S(1)}, f32[8,2,256,128]{3,2,1,0:T(8,128)S(1)}) %tuple.55, (pred[256,512]{0,1:T(8,128)(4,1)S(1)}, ...), branch_computations={%region_6.6_spmd, %region_7.9_spmd} | conditional | flops 1102061568 | bytes 33162272 | solution.py:120
  60.6 2.6 %fusion = (f32[8,2,256]{2,1,0:T(2,128)S(1)}, f32[8,512,256,2]{2,1,3,0:T(8,128)S(1)}) fusion(pred[256,512]{0,1:T(8,128)(4,1)S(1)} %get-tuple-element.199, bf16[8,256,2,128]{3,1,2,0:T(8,128)(2,1)S(1)} %get-tuple-element.202, bf16[8,1536,128]{2,1,0:T(8,128)(2,1)} %get-tuple-element.200, s32[]{:T(128)} %get-tuple-element.201), kind=kOutput, calls=%fused_computation.2 | convolution fusion | flops 543158272 | bytes 10633728 | tf_op jit(solution)/shard_map/while/body/eval_jaxpr/cond/branch_1_fun/ktgd,kud->kgtu/dot_general | solution.py:99
  63.2 2.0 %fusion.2 = f32[8,2,256]{2,1,0:T(2,128)S(1)} fusion(f32[8,512,256,2]{2,1,3,0:T(8,128)S(1)} %get-tuple-element.249, f32[8,2,256]{2,1,0:T(2,128)S(1)} %max.4, pred[256,512]{0,1:T(8,128)(4,1)S(1)} %get-tuple-element.199), kind=kLoop, calls=%fused_computation.4 | loop fusion | flops 10481664 | bytes 8552448 | tf_op jit(solution)/shard_map/while/body/eval_jaxpr/cond/branch_1_fun/reduce_sum | solution.py:108
  65.3 4.4 %multiply_add_fusion = f32[8,2,256,128]{3,2,1,0:T(8,128)S(1)} fusion(f32[8,2,256,128]{3,2,1,0:T(8,128)S(1)} %get-tuple-element.204, f32[8,512,256,2]{2,1,3,0:T(8,128)S(1)} %get-tuple-element.249, f32[8,2,256]{2,1,0:T(2,128)S(1)} %max.4, pred[256,512]{0,1:T(8,128)(4,1)S(1)} %get-tuple-element.199, bf16[8,1536,128]{2,1,0:T(8,128)(2,1)} %get-tuple-element.205, ...), kind=kOutput, calls=%fused_computation.7 | convolution fusion | flops 548405248 | bytes 13795840 | tf_op jit(solution)/shard_map/while/body/eval_jaxpr/cond/branch_1_fun/kgtu,kud->kgtd/dot_general | solution.py:109
  72.1 9.1 %conditional.2 = ((f32[8,2,256]{2,1,0:T(2,128)S(1)}, f32[8,2,256]{2,1,0:T(2,128)S(1)}, f32[8,2,256,128]{3,2,1,0:T(8,128)S(1)})) conditional(s32[]{:T(128)} %convert_element_type.83, (f32[8,2,256]{2,1,0:T(2,128)S(1)}, f32[8,2,256]{2,1,0:T(2,128)S(1)}, f32[8,2,256,128]{3,2,1,0:T(8,128)S(1)}) %tuple.55, (pred[256,512]{0,1:T(8,128)(4,1)S(1)}, ...), branch_computations={%region_6.6_spmd, %region_7.9_spmd} | conditional | flops 1102061568 | bytes 33162272 | solution.py:120
  72.1 2.6 %fusion = (f32[8,2,256]{2,1,0:T(2,128)S(1)}, f32[8,512,256,2]{2,1,3,0:T(8,128)S(1)}) fusion(pred[256,512]{0,1:T(8,128)(4,1)S(1)} %get-tuple-element.199, bf16[8,256,2,128]{3,1,2,0:T(8,128)(2,1)S(1)} %get-tuple-element.202, bf16[8,1536,128]{2,1,0:T(8,128)(2,1)} %get-tuple-element.200, s32[]{:T(128)} %get-tuple-element.201), kind=kOutput, calls=%fused_computation.2 | convolution fusion | flops 543158272 | bytes 10633728 | tf_op jit(solution)/shard_map/while/body/eval_jaxpr/cond/branch_1_fun/ktgd,kud->kgtu/dot_general | solution.py:99
  74.7 2.0 %fusion.2 = f32[8,2,256]{2,1,0:T(2,128)S(1)} fusion(f32[8,512,256,2]{2,1,3,0:T(8,128)S(1)} %get-tuple-element.249, f32[8,2,256]{2,1,0:T(2,128)S(1)} %max.4, pred[256,512]{0,1:T(8,128)(4,1)S(1)} %get-tuple-element.199), kind=kLoop, calls=%fused_computation.4 | loop fusion | flops 10481664 | bytes 8552448 | tf_op jit(solution)/shard_map/while/body/eval_jaxpr/cond/branch_1_fun/reduce_sum | solution.py:108
  76.8 4.4 %multiply_add_fusion = f32[8,2,256,128]{3,2,1,0:T(8,128)S(1)} fusion(f32[8,2,256,128]{3,2,1,0:T(8,128)S(1)} %get-tuple-element.204, f32[8,512,256,2]{2,1,3,0:T(8,128)S(1)} %get-tuple-element.249, f32[8,2,256]{2,1,0:T(2,128)S(1)} %max.4, pred[256,512]{0,1:T(8,128)(4,1)S(1)} %get-tuple-element.199, bf16[8,1536,128]{2,1,0:T(8,128)(2,1)} %get-tuple-element.205, ...), kind=kOutput, calls=%fused_computation.7 | convolution fusion | flops 548405248 | bytes 13795840 | tf_op jit(solution)/shard_map/while/body/eval_jaxpr/cond/branch_1_fun/kgtu,kud->kgtd/dot_general | solution.py:109
  83.6 9.1 %conditional.2 = ((f32[8,2,256]{2,1,0:T(2,128)S(1)}, f32[8,2,256]{2,1,0:T(2,128)S(1)}, f32[8,2,256,128]{3,2,1,0:T(8,128)S(1)})) conditional(s32[]{:T(128)} %convert_element_type.83, (f32[8,2,256]{2,1,0:T(2,128)S(1)}, f32[8,2,256]{2,1,0:T(2,128)S(1)}, f32[8,2,256,128]{3,2,1,0:T(8,128)S(1)}) %tuple.55, (pred[256,512]{0,1:T(8,128)(4,1)S(1)}, ...), branch_computations={%region_6.6_spmd, %region_7.9_spmd} | conditional | flops 1102061568 | bytes 33162272 | solution.py:120
  83.6 2.6 %fusion = (f32[8,2,256]{2,1,0:T(2,128)S(1)}, f32[8,512,256,2]{2,1,3,0:T(8,128)S(1)}) fusion(pred[256,512]{0,1:T(8,128)(4,1)S(1)} %get-tuple-element.199, bf16[8,256,2,128]{3,1,2,0:T(8,128)(2,1)S(1)} %get-tuple-element.202, bf16[8,1536,128]{2,1,0:T(8,128)(2,1)} %get-tuple-element.200, s32[]{:T(128)} %get-tuple-element.201), kind=kOutput, calls=%fused_computation.2 | convolution fusion | flops 543158272 | bytes 10633728 | tf_op jit(solution)/shard_map/while/body/eval_jaxpr/cond/branch_1_fun/ktgd,kud->kgtu/dot_general | solution.py:99
  86.2 2.0 %fusion.2 = f32[8,2,256]{2,1,0:T(2,128)S(1)} fusion(f32[8,512,256,2]{2,1,3,0:T(8,128)S(1)} %get-tuple-element.249, f32[8,2,256]{2,1,0:T(2,128)S(1)} %max.4, pred[256,512]{0,1:T(8,128)(4,1)S(1)} %get-tuple-element.199), kind=kLoop, calls=%fused_computation.4 | loop fusion | flops 10481664 | bytes 8552448 | tf_op jit(solution)/shard_map/while/body/eval_jaxpr/cond/branch_1_fun/reduce_sum | solution.py:108
  88.3 4.4 %multiply_add_fusion = f32[8,2,256,128]{3,2,1,0:T(8,128)S(1)} fusion(f32[8,2,256,128]{3,2,1,0:T(8,128)S(1)} %get-tuple-element.204, f32[8,512,256,2]{2,1,3,0:T(8,128)S(1)} %get-tuple-element.249, f32[8,2,256]{2,1,0:T(2,128)S(1)} %max.4, pred[256,512]{0,1:T(8,128)(4,1)S(1)} %get-tuple-element.199, bf16[8,1536,128]{2,1,0:T(8,128)(2,1)} %get-tuple-element.205, ...), kind=kOutput, calls=%fused_computation.7 | convolution fusion | flops 548405248 | bytes 13795840 | tf_op jit(solution)/shard_map/while/body/eval_jaxpr/cond/branch_1_fun/kgtu,kud->kgtd/dot_general | solution.py:109
  93.3 40.5 %psum.7 = f32[]{:T(128)} all-reduce(f32[]{:T(128)} %multiply_reduce_fusion), channel_id=1, replica_groups=mesh['dp'=4,'seq'=8] {'dp','seq'}, use_global_device_ids=true, to_apply=%region_12.13 | all-reduce | flops 1 | bytes 8 | tf_op jit(solution)/shard_map/psum | solution.py:136
  134.5 2.0 %copy.17 = bf16[256,8,2,128]{3,2,1,0:T(2,128)(2,1)} copy(bf16[256,8,2,128]{3,0,2,1:T(8,128)(2,1)S(1)} %fusion.20) | data formatting | bytes 2097152 | tf_op jit(solution)/shard_map/convert_element_type | solution.py:133
  (52 shorter events, 20.4 us)
Async XLA Ops:
  4.0 3.6 %copy-start = (bf16[1,256,8,128]{3,2,1,0:T(8,128)(2,1)S(1)}, bf16[1,256,8,128]{3,2,1,0:T(8,128)(2,1)}, u32[]{:S(2)}) copy-start(bf16[1,256,8,128]{3,2,1,0:T(8,128)(2,1)} %param.10) | copy-start | bytes 1572868
  4.4 19.6 %copy-start.1 = (bf16[1,256,16,128]{3,2,1,0:T(8,128)(2,1)S(1)}, bf16[1,256,16,128]{3,2,1,0:T(8,128)(2,1)}, u32[]{:S(2)}) copy-start(bf16[1,256,16,128]{3,2,1,0:T(8,128)(2,1)} %param.8) | copy-start | bytes 3145732
  5.6 10.5 %collective-permute-start = (bf16[8,256,128]{2,1,0:T(8,128)(2,1)S(1)}, bf16[8,256,128]{2,1,0:T(8,128)(2,1)S(1)}, u32[]{:S(2)}, u32[]{:S(2)}) collective-permute-start(bf16[8,256,128]{2,1,0:T(8,128)(2,1)S(1)} %get-tuple-element.247), channel_id=1, source_target_pairs={{0,1},{1,2},{2,3},{3,4},{4,5},{5,6},{6,7},{8,9},{9,10},{10,11},{11... | collective-permute-start | bytes 1572872 | tf_op jit(solution)/shard_map/ppermute | solution.py:17
  7.6 14.1 %collective-permute-start.4 = (bf16[8,256,128]{2,1,0:T(8,128)(2,1)S(1)}, bf16[8,256,128]{2,1,0:T(8,128)(2,1)S(1)}, u32[]{:S(2)}, u32[]{:S(2)}) collective-permute-start(bf16[8,256,128]{2,1,0:T(8,128)(2,1)S(1)} %bitcast.71), channel_id=1, source_target_pairs={{0,1},{1,2},{2,3},{3,4},{4,5},{5,6},{6,7},{8,9},{9,10},{10,11},{11... | collective-permute-start | bytes 1572872 | tf_op jit(solution)/shard_map/ppermute | solution.py:17
  16.1 11.2 %collective-permute-start.1 = (bf16[8,256,128]{2,1,0:T(8,128)(2,1)S(1)}, bf16[8,256,128]{2,1,0:T(8,128)(2,1)S(1)}, u32[]{:S(2)}, u32[]{:S(2)}) collective-permute-start(bf16[8,256,128]{2,1,0:T(8,128)(2,1)S(1)} %collective-permute-done), channel_id=1, source_target_pairs={{0,1},{1,2},{2,3},{3,4},{4,5},{5,6},{6,7},{8,9},{9,10},{10,11},{11... | collective-permute-start | bytes 1572872 | tf_op jit(solution)/shard_map/ppermute | solution.py:17
  21.7 11.3 %collective-permute-start.5 = (bf16[8,256,128]{2,1,0:T(8,128)(2,1)S(1)}, bf16[8,256,128]{2,1,0:T(8,128)(2,1)}, u32[]{:S(2)}, u32[]{:S(2)}) collective-permute-start(bf16[8,256,128]{2,1,0:T(8,128)(2,1)S(1)} %collective-permute-done.4), channel_id=1, source_target_pairs={{0,1},{1,2},{2,3},{3,4},{4,5},{5,6},{6,7},{8,9},{9,10},{10,11},{11... | collective-permute-start | bytes 1572872 | tf_op jit(solution)/shard_map/ppermute | solution.py:17
  27.4 11.3 %collective-permute-start.2 = (bf16[8,256,128]{2,1,0:T(8,128)(2,1)S(1)}, bf16[8,256,128]{2,1,0:T(8,128)(2,1)}, u32[]{:S(2)}, u32[]{:S(2)}) collective-permute-start(bf16[8,256,128]{2,1,0:T(8,128)(2,1)S(1)} %collective-permute-done.1), channel_id=1, source_target_pairs={{0,1},{1,2},{2,3},{3,4},{4,5},{5,6},{6,7},{8,9},{9,10},{10,11},{11... | collective-permute-start | bytes 1572872 | tf_op jit(solution)/shard_map/ppermute | solution.py:17
  33.1 11.2 %collective-permute-start.6 = (bf16[8,256,128]{2,1,0:T(8,128)(2,1)}, bf16[8,256,128]{2,1,0:T(8,128)(2,1)}, u32[]{:S(2)}, u32[]{:S(2)}) collective-permute-start(bf16[8,256,128]{2,1,0:T(8,128)(2,1)} %collective-permute-done.5), channel_id=1, source_target_pairs={{0,1},{1,2},{2,3},{3,4},{4,5},{5,6},{6,7},{8,9},{9,10},{10,11},{11... | collective-permute-start | bytes 1572872 | tf_op jit(solution)/shard_map/ppermute | solution.py:17
  38.7 12.6 %collective-permute-start.3 = (bf16[8,256,128]{2,1,0:T(8,128)(2,1)}, bf16[8,256,128]{2,1,0:T(8,128)(2,1)S(1)}, u32[]{:S(2)}, u32[]{:S(2)}) collective-permute-start(bf16[8,256,128]{2,1,0:T(8,128)(2,1)} %collective-permute-done.2), channel_id=1, source_target_pairs={{0,1},{1,2},{2,3},{3,4},{4,5},{5,6},{6,7},{8,9},{9,10},{10,11},{11... | collective-permute-start | bytes 1572872 | tf_op jit(solution)/shard_map/ppermute | solution.py:17
  44.3 11.6 %collective-permute-start.7 = (bf16[8,256,128]{2,1,0:T(8,128)(2,1)}, bf16[8,256,128]{2,1,0:T(8,128)(2,1)S(1)}, u32[]{:S(2)}, u32[]{:S(2)}) collective-permute-start(bf16[8,256,128]{2,1,0:T(8,128)(2,1)} %collective-permute-done.6), channel_id=1, source_target_pairs={{0,1},{1,2},{2,3},{3,4},{4,5},{5,6},{6,7},{8,9},{9,10},{10,11},{11... | collective-permute-start | bytes 1572872 | tf_op jit(solution)/shard_map/ppermute | solution.py:17
where the time goes:
time: 141 us; the launch traced here: 138 us
  blocking collectives  40.5 us (29%)
  other arithmetic  21.6 us (15%)
  matrix products  20.9 us (15%)
  waiting for transfers between devices  17.6 us (12%)
  starting transfers between devices  17.3 us (12%)
  local copies, waits for them, and re-layouts  15.6 us (11%)
  between operations  2.67 us (2%)
  loops' own time  2.19 us (2%)
    psum x1, blocking collectives, shards(): all_squares = lax.psum(local_squares, ('dp', 'seq'))  40.5 us
    ppermute x8, waiting for transfers between devices, shifted(): return lax.ppermute(block, axis, route)  17.6 us
    ppermute x8, starting transfers between devices, shifted(): return lax.ppermute(block, axis, route)  17.3 us
    dot_general x3, matrix products, update(): jnp.einsum('kgtu,kud->kgtd', weights.astype(jnp.bfloat16), values_step, p...  13.1 us
    dot_general x3, matrix products, update(): jnp.einsum('ktgd,kud->kgtu', grouped, keys_step, preferred_element_type=j...  7.83 us
    unnamed x12, local copies, waits for them, and re-layouts  6.16 us
    reduce_sum x3, other arithmetic, update(): new_total = old_total * rescale + jnp.sum(weights, axis=-1)  6.06 us
    reduce_or x3, other arithmetic, visit(): return lax.cond(jnp.any(visible_step), update, unchanged, carry)  5.23 us
  transfers between devices with their start and end apart: 8, of which 6 were waited for; matrix products, arithmetic and copies ran while one was open for 11% of the time, Pallas kernels for 0%

commit v1 on v0

v1 whole, which is shorter than its diff:
```python
import functools
import math

import jax
import jax.numpy as jnp
import numpy as np
from jax import lax
from jax.experimental import pallas as pl
from jax.experimental.pallas import tpu as pltpu
from jax.sharding import PartitionSpec as P

WINDOW = 1024
rope_base = 500000.0
score_scale = 1.0 / 12.0
masked = -1e30
MESH = pl.DeviceIdType.MESH
CHUNKS = 4


def tables(rows, reach, width):
    half = width // 2
    frequency = rope_base ** (-2.0 * np.arange(half) / width)
    at = np.arange(rows)[None, :] - rows * np.arange(reach + 1)[:, None]
    angles = at[..., None] * frequency
    cos = np.concatenate([np.cos(angles)] * 2, axis=-1)
    sin = np.concatenate([-np.sin(angles), np.sin(angles)], axis=-1)
    return np.stack([cos, sin], axis=1).astype(np.float32)


def body(
    n, n_dp, reach, lengths, q_hbm, k_hbm, v_hbm, tab, out, z_out,
    q_raw, raw, stage, q_rot, weights, peaks, totals, acc, low, bias, mine, parts_seq, mine2, parts_dp,
    load_sem, z_send, z_recv, d_send, d_recv, s_send, s_recv, p_send, p_recv,
):
    rows, heads, width = k_hbm.shape
    q_heads = q_hbm.shape[1]
    group = q_heads // heads
    hops = reach // 2
    piece = rows // CHUNKS
    me = lax.axis_index("seq")
    dp = lax.axis_index("dp")
    core = lax.rem(me, 2)
    chip = me // 2
    other = me + 1 - 2 * core
    above = me + 2
    has_above = above < n
    first = core == 0
    second = core == 1

    loads = [
        pltpu.make_async_copy(k_hbm, raw.at[0, 0], load_sem.at[0]),
        pltpu.make_async_copy(v_hbm, raw.at[1, 0], load_sem.at[1]),
        pltpu.make_async_copy(q_hbm, q_raw, load_sem.at[2]),
    ]
    for load in loads:
        load.start()

    barrier = pltpu.get_barrier_semaphore()

    def greet_seq(j, _):
        pl.semaphore_signal(barrier, inc=1, device_id={"seq": lax.rem(me + j, n)}, device_id_type=MESH)
        return 0

    def greet_dp(j, _):
        pl.semaphore_signal(barrier, inc=1, device_id={"dp": lax.rem(dp + j, n_dp)}, device_id_type=MESH)
        return 0

    lax.fori_loop(1, n, greet_seq, 0)
    lax.fori_loop(1, n_dp, greet_dp, 0)

    peaks[...] = jnp.full_like(peaks, masked)
    totals[...] = jnp.zeros_like(totals)
    acc[...] = jnp.zeros_like(acc)
    row_at = me * rows + lax.broadcasted_iota(jnp.int32, (rows, width), 0)
    start = jnp.zeros((rows, width), jnp.int32)
    end = jnp.int32(0)
    for i in range(lengths.shape[1]):
        end = end + lengths[0, i]
        start = jnp.where(end <= row_at, end, start)
    low[...] = jnp.maximum(start, row_at - (WINDOW - 1)) - me * rows

    for load in loads:
        load.wait()
    pl.semaphore_wait(barrier, (n - 1) + (n_dp - 1))

    def up(kind, hop, i):
        return pltpu.make_async_remote_copy(
            src_ref=raw.at[kind, 2 * hop, pl.ds(i * piece, piece)],
            dst_ref=raw.at[kind, 2 * hop + 2, pl.ds(i * piece, piece)],
            send_sem=z_send.at[kind, hop, i],
            recv_sem=z_recv.at[kind, hop, i],
            device_id={"seq": above},
            device_id_type=MESH,
        )

    def across(kind, hop, i):
        there = 2 * hop + 1 - 2 * core
        slot = hop - core
        return pltpu.make_async_remote_copy(
            src_ref=raw.at[kind, 2 * hop, pl.ds(i * piece, piece)],
            dst_ref=raw.at[kind, there, pl.ds(i * piece, piece)],
            send_sem=d_send.at[kind, slot, i],
            recv_sem=d_recv.at[kind, slot, i],
            device_id={"seq": other},
            device_id_type=MESH,
        )

    def each(low_i, high_i, do):
        def step(i, _):
            do(i)
            return 0

        lax.fori_loop(low_i, high_i, step, 0)

    def send_up(kind, hop, a, b):
        @pl.when(has_above)
        def _():
            each(a, b, lambda i: up(kind, hop, i).start())

    send_up(0, 0, 0, CHUNKS)
    send_up(1, 0, 0, 1)

    @pl.when(first)
    def _():
        for kind in range(2):
            each(0, CHUNKS, lambda i: across(kind, 0, i).start())

    def take(kind, hop, a, b):
        def one(i):
            up(kind, hop - 1, i).wait_recv()
            if hop < hops:
                @pl.when(has_above)
                def _():
                    up(kind, hop, i).start()

                across(kind, hop, i).start()
            else:
                @pl.when(second)
                def _():
                    across(kind, hop, i).start()

        each(a, b, one)

    def take_across(kind, slot, a, b):
        def one(i):
            pltpu.make_async_remote_copy(
                src_ref=raw.at[kind, 0, pl.ds(i * piece, piece)],
                dst_ref=raw.at[kind, 2 * slot + 1, pl.ds(i * piece, piece)],
                send_sem=d_send.at[kind, slot, i],
                recv_sem=d_recv.at[kind, slot, i],
                device_id={"seq": other},
                device_id_type=MESH,
            ).wait_recv()

        each(a, b, one)

    stage[...] = q_raw[...].astype(jnp.float32).reshape(rows * q_heads, width)
    scale = score_scale * math.log2(math.e)

    def turn_q(h, _):
        for g in range(group):
            x = stage[pl.ds(h * group + g, rows, stride=q_heads), :]
            turned = x * tab[0, 0] + pltpu.roll(x, width // 2, 1) * tab[0, 1]
            q_rot[h, g * rows : (g + 1) * rows, :] = (turned * scale).astype(jnp.bfloat16)
        return 0

    lax.fori_loop(0, heads, turn_q, 0)

    lane = lax.broadcasted_iota(jnp.int32, (rows, width), 1)

    def score(d):
        stage[0 : rows * heads, :] = raw[0, d].astype(jnp.float32).reshape(rows * heads, width)
        key_at = lax.broadcasted_iota(jnp.int32, (rows, rows), 1) - d * rows
        query_at = lax.broadcasted_iota(jnp.int32, (rows, rows), 0)
        seen = (key_at >= low[:, 0:1]) & (key_at <= query_at)
        bias[...] = jnp.where(seen, 0.0, masked)

        def head(h, _):
            x = stage[pl.ds(h, rows, stride=heads), :]
            k = (x * tab[d, 0] + pltpu.roll(x, width // 2, 1) * tab[d, 1]).astype(jnp.bfloat16)
            for g in range(group):
                part = slice(g * rows, (g + 1) * rows)
                s = lax.dot_general(
                    q_rot[h, part, :], k, (((1,), (1,)), ((), ())), preferred_element_type=jnp.float32
                )
                s = s + bias[...]
                m = jnp.max(s, axis=1, keepdims=True)
                p = jnp.exp2(s - m)
                t = jnp.sum(p, axis=1, keepdims=True)
                weights[d, h, part, :] = p.astype(jnp.bfloat16)
                peaks[h, part, :] = jnp.where(lane == d, m, peaks[h, part, :])
                totals[h, part, :] = jnp.where(lane == d, t, totals[h, part, :])
            return 0

        lax.fori_loop(0, heads, head, 0)

    def mix(d, a, b):
        count = b - a
        stage[0 : count * heads, :] = raw[1, d, a:b].astype(jnp.float32).reshape(count * heads, width)

        def head(h, _):
            v = stage[pl.ds(h, count, stride=heads), :].astype(jnp.bfloat16)
            o = jnp.dot(weights[d, h, :, a:b], v, preferred_element_type=jnp.float32)
            acc[h] = acc[h] + peaks[h, :, d : d + 1] * o
            return 0

        lax.fori_loop(0, heads, head, 0)

    score(0)

    @pl.when(second)
    def _():
        take_across(0, 0, 0, CHUNKS)
        score(1)

    @pl.when(chip >= 1)
    def _():
        take(0, 1, 0, CHUNKS)

    send_up(1, 0, 1, CHUNKS)

    @pl.when(chip >= 1)
    def _():
        score(2)
        take_across(0, core, 0, CHUNKS)
        score(1 + 2 * core)
        take(1, 1, 0, 1)

    @pl.when(chip >= 2)
    def _():
        take(0, 2, 0, CHUNKS)
        score(4)

        @pl.when(first)
        def _():
            take_across(0, 1, 0, CHUNKS)
            score(3)

    def settle(h, square):
        m = peaks[h]
        peak = jnp.max(m, axis=1, keepdims=True)
        a = jnp.exp2(m - peak)
        total = jnp.sum(a * totals[h], axis=1, keepdims=True)
        peaks[h] = a / total
        lse = peak * math.log(2.0) + jnp.log(total)
        return square + jnp.sum(lse * lse, axis=0, keepdims=True)

    square = lax.fori_loop(0, heads, settle, jnp.zeros((1, 1), jnp.float32))
    mine[...] = jnp.broadcast_to(square, mine.shape)
    parts_seq[me] = jnp.broadcast_to(square, mine.shape)

    mix(0, 0, rows)

    def tell_seq(j):
        return pltpu.make_async_remote_copy(
            src_ref=mine, dst_ref=parts_seq.at[me], send_sem=s_send.at[j], recv_sem=s_recv.at[j],
            device_id={"seq": lax.rem(me + j, n)}, device_id_type=MESH,
        )

    def heard_seq(j):
        return pltpu.make_async_remote_copy(
            src_ref=mine, dst_ref=parts_seq.at[lax.rem(me + n - j, n)], send_sem=s_send.at[j], recv_sem=s_recv.at[j],
            device_id={"seq": lax.rem(me + j, n)}, device_id_type=MESH,
        )

    def tell_dp(j):
        return pltpu.make_async_remote_copy(
            src_ref=mine2, dst_ref=parts_dp.at[dp], send_sem=p_send.at[j], recv_sem=p_recv.at[j],
            device_id={"dp": lax.rem(dp + j, n_dp)}, device_id_type=MESH,
        )

    def heard_dp(j):
        return pltpu.make_async_remote_copy(
            src_ref=mine2, dst_ref=parts_dp.at[lax.rem(dp + n_dp - j, n_dp)], send_sem=p_send.at[j], recv_sem=p_recv.at[j],
            device_id={"dp": lax.rem(dp + j, n_dp)}, device_id_type=MESH,
        )

    each(1, n, lambda j: tell_seq(j).start())

    @pl.when(second)
    def _():
        take_across(1, 0, 0, CHUNKS)
        mix(1, 0, rows)

    @pl.when(chip >= 1)
    def _():
        take(1, 1, 1, CHUNKS)
        mix(2, 0, rows)

        @pl.when(first)
        def _():
            take_across(1, 0, 0, CHUNKS)
            mix(1, 0, rows)

        @pl.when(second)
        def _():
            take_across(1, 1, 0, CHUNKS)
            mix(3, 0, rows)

    each(1, n, lambda j: heard_seq(j).wait_recv())
    column = jnp.sum(parts_seq[...], axis=0)
    mine2[...] = column
    parts_dp[dp] = column

    middle = rows // 2

    @pl.when(chip >= 2)
    def _():
        take(1, 2, 0, CHUNKS // 2)
        mix(4, 0, middle)

        @pl.when(first)
        def _():
            take_across(1, 1, 0, CHUNKS // 2)
            mix(3, 0, middle)

    each(1, n_dp, lambda j: tell_dp(j).start())
    each(1, n_dp, lambda j: heard_dp(j).wait_recv())
    z_out[0, 0] = jnp.sum(jnp.sum(parts_dp[...], axis=0)[0:1, 0:1]) / (n_dp * n * rows * q_heads)

    @pl.when(chip >= 2)
    def _():
        take(1, 2, CHUNKS // 2, CHUNKS)
        mix(4, middle, rows)

        @pl.when(first)
        def _():
            take_across(1, 1, CHUNKS // 2, CHUNKS)
            mix(3, middle, rows)

    def give(h, _):
        for g in range(group):
            stage[pl.ds(h * group + g, rows, stride=q_heads), :] = acc[h, g * rows : (g + 1) * rows, :]
        return 0

    lax.fori_loop(0, heads, give, 0)
    out[...] = stage[...].reshape(rows, q_heads, width).astype(jnp.bfloat16)

    def sent_up(kind, hop):
        each(0, CHUNKS, lambda i: up(kind, hop, i).wait_send())

    def sent_across(kind, hop):
        each(0, CHUNKS, lambda i: across(kind, hop, i).wait_send())

    for kind in range(2):
        pl.when(has_above)(functools.partial(sent_up, kind, 0))
        pl.when(has_above & (chip >= 1))(functools.partial(sent_up, kind, 1))
        pl.when(first)(functools.partial(sent_across, kind, 0))
        pl.when(chip >= 1)(functools.partial(sent_across, kind, 1))
        pl.when(second & (chip >= 2))(functools.partial(sent_across, kind, 2))
    each(1, n, lambda j: tell_seq(j).wait_send())
    each(1, n_dp, lambda j: tell_dp(j).wait_send())


def shards(queries, keys, values, doc_lengths):
    _, rows, q_heads, width = queries.shape
    heads = keys.shape[2]
    group = q_heads // heads
    n = lax.axis_size("seq")
    n_dp = lax.axis_size("dp")
    reach = -(-(WINDOW - 1) // rows)
    assert n % 2 == 0 and reach == 4
    hops = reach // 2
    tab = jnp.asarray(tables(rows, reach, width))
    vmem = pl.BlockSpec(memory_space=pltpu.VMEM)
    smem = pl.BlockSpec(memory_space=pltpu.SMEM)
    anywhere = pl.BlockSpec(memory_space=pl.ANY)
    dma = pltpu.SemaphoreType.DMA
    out, z = pl.pallas_call(
        functools.partial(body, n, n_dp, reach),
        out_shape=(
            jax.ShapeDtypeStruct((rows, q_heads, width), jnp.bfloat16),
            jax.ShapeDtypeStruct((1, 1), jnp.float32),
        ),
        in_specs=[smem, anywhere, anywhere, anywhere, vmem],
        out_specs=(vmem, smem),
        scratch_shapes=[
            pltpu.VMEM((rows, q_heads, width), jnp.bfloat16),
            pltpu.VMEM((2, reach + 1, rows, heads, width), jnp.bfloat16),
            pltpu.VMEM((rows * q_heads, width), jnp.float32),
            pltpu.VMEM((heads, group * rows, width), jnp.bfloat16),
            pltpu.VMEM((reach + 1, heads, group * rows, rows), jnp.bfloat16),
            pltpu.VMEM((heads, group * rows, width), jnp.float32),
            pltpu.VMEM((heads, group * rows, width), jnp.float32),
            pltpu.VMEM((heads, group * rows, width), jnp.float32),
            pltpu.VMEM((rows, width), jnp.int32),
            pltpu.VMEM((rows, rows), jnp.float32),
            pltpu.VMEM((8, width), jnp.float32),
            pltpu.VMEM((n, 8, width), jnp.float32),
            pltpu.VMEM((8, width), jnp.float32),
            pltpu.VMEM((n_dp, 8, width), jnp.float32),
            dma((3,)),
            dma((2, hops, CHUNKS)),
            dma((2, hops, CHUNKS)),
            dma((2, hops, CHUNKS)),
            dma((2, hops, CHUNKS)),
            dma((n,)),
            dma((n,)),
            dma((n_dp,)),
            dma((n_dp,)),
        ],
        compiler_params=pltpu.CompilerParams(
            collective_id=0, has_side_effects=True, vmem_limit_bytes=60 * 1024 * 1024
        ),
        name="attend",
    )(doc_lengths, queries[0], keys[0], values[0], tab)
    return out[None], z[0, 0]


def solution(mesh):
    placed = (
        P("dp", "seq", None, None),
        P("dp", "seq", None, None),
        P("dp", "seq", None, None),
        P("dp", None),
    )
    return jax.shard_map(
        shards,
        mesh=mesh,
        in_specs=placed,
        out_specs=(P("dp", "seq", None, None), P()),
        check_vma=False,
    )
```

time: 141 us -> 66.5 us (0.47); the launches traced: 138 us -> 66.3 us
  Pallas kernels: 0 us -> 61.6 us
  blocking collectives: 40.5 us -> 0 us
  other arithmetic: 21.6 us -> 0 us
  matrix products: 20.9 us -> 0 us
  waiting for transfers between devices: 17.6 us -> 0 us
  starting transfers between devices: 17.3 us -> 0 us
  local copies, waits for them, and re-layouts: 15.6 us -> 2.37 us
  loops' own time: 2.19 us -> 0 us
    pallas_call x0 -> x1, Pallas kernels: none -> 61.6 us  [shards(): pl.pallas_call(functools.partial(body, n, n_dp, reach), out_shape=(jax.Sh...]
    psum x1 -> x0, blocking collectives: 40.5 us -> none  [shards(): all_squares = lax.psum(local_squares, ('dp', 'seq'))]
    dot_general x6 -> x0, matrix products: 20.9 us -> none  [the longest x3 13.1 us: update(): jnp.einsum('kgtu,kud->kgtd', weights.astype(jnp.bfloat16), values_step, p...]
    ppermute x8 -> x0, waiting for transfers between devices: 17.6 us -> none  [shifted(): return lax.ppermute(block, axis, route)]
    ppermute x8 -> x0, starting transfers between devices: 17.3 us -> none  [shifted(): return lax.ppermute(block, axis, route)]
    reduce_sum x7 -> x0, other arithmetic: 6.95 us -> none  [the longest x3 6.06 us: update(): new_total = old_total * rescale + jnp.sum(weights, axis=-1)]
    pad x2 -> x0, local copies, waits for them, and re-layouts: 5.66 us -> none  [the longest x1 3.69 us: shards(): padded_keys = jnp.pad(near_keys, ((0, 0), (0, extra_rows), (0, 0)))]
    reduce_or x3 -> x0, other arithmetic: 5.23 us -> none  [visit(): return lax.cond(jnp.any(visible_step), update, unchanged, carry)]
  transfers between devices with their start and end apart: 8 -> 0, of which waited for: 6 -> 0; matrix products, arithmetic and copies ran while one was open for 11% -> 0% of each run, Pallas kernels for 0% -> 0%
where the time goes in v1:
time: 66.5 us; the launch traced here: 66.3 us
  Pallas kernels  61.6 us (93%)
  local copies, waits for them, and re-layouts  2.37 us (4%)
  between operations  2.33 us (4%)
    pallas_call x1, Pallas kernels, shards(): pl.pallas_call(functools.partial(body, n, n_dp, reach), out_shape=(jax.Sh...  61.6 us
    unnamed x1, local copies, waits for them, and re-layouts  2.37 us

profile of v1, /device:TPU:16, one launch (start us, length us, event | category | flops | bytes accessed | tf_op | source)
XLA Modules:
  0.0 66.3 jit_solution(13745670838530841132)
XLA Ops:
  0.6 61.6 %attend.1 = (bf16[256,16,128]{2,1,0:T(8,128)(2,1)}, f32[1,1]{1,0:T(1,128)}) custom-call(s32[1,8]{1,0:T(1,128)} %lengths.1, bf16[256,16,128]{2,1,0:T(8,128)(2,1)} %bitcast.5, bf16[256,8,128]{2,1,0:T(8,128)(2,1)} %bitcast.7, bf16[256,8,128]{2,1,0:T(8,128)(2,1)} %bitcast.8, f32[5,2,256,128]{3,2,1,0:T(8,128)} %constant.2.clone.tab), custom_call_target="tpu_custom_call" | custom-call | tf_op jit(solution)/shard_map/attend/pallas_call | solution.py:369
  62.2 2.4 %copy.9 = bf16[1,256,16,128]{3,2,1,0:T(8,128)(2,1)} copy(bf16[1,256,16,128]{3,2,1,0:T(8,128)(2,1)} %bitcast.6) | data formatting | bytes 2097152

commit v2 on v1

--- a/solution.py
+++ b/solution.py
@@ -15,6 +15,7 @@
 masked = -1e30
 MESH = pl.DeviceIdType.MESH
 CHUNKS = 4
+UNROLL = 2
 
 
 def tables(rows, reach, width):
@@ -28,8 +29,8 @@
 
 
 def body(
-    n, n_dp, reach, lengths, q_hbm, k_hbm, v_hbm, tab, out, z_out,
-    q_raw, raw, stage, q_rot, weights, peaks, totals, acc, low, bias, mine, parts_seq, mine2, parts_dp,
+    n, n_dp, reach, lengths, q_hbm, k_hbm, v_hbm, tab_hbm, out, z_out,
+    tab, q_raw, raw, stage, spread, q_rot, weights, peaks, totals, acc, low, bias, mine, parts_seq, mine2, parts_dp,
     load_sem, z_send, z_recv, d_send, d_recv, s_send, s_recv, p_send, p_recv,
 ):
     rows, heads, width = k_hbm.shape
@@ -51,6 +52,7 @@
         pltpu.make_async_copy(k_hbm, raw.at[0, 0], load_sem.at[0]),
         pltpu.make_async_copy(v_hbm, raw.at[1, 0], load_sem.at[1]),
         pltpu.make_async_copy(q_hbm, q_raw, load_sem.at[2]),
+        pltpu.make_async_copy(tab_hbm, tab, load_sem.at[3]),
     ]
     for load in loads:
         load.start()
@@ -70,7 +72,6 @@
 
     peaks[...] = jnp.full_like(peaks, masked)
     totals[...] = jnp.zeros_like(totals)
-    acc[...] = jnp.zeros_like(acc)
     row_at = me * rows + lax.broadcasted_iota(jnp.int32, (rows, width), 0)
     start = jnp.zeros((rows, width), jnp.int32)
     end = jnp.int32(0)
@@ -79,8 +80,8 @@
         start = jnp.where(end <= row_at, end, start)
     low[...] = jnp.maximum(start, row_at - (WINDOW - 1)) - me * rows
 
-    for load in loads:
-        load.wait()
+    loads[0].wait()
+    loads[1].wait()
     pl.semaphore_wait(barrier, (n - 1) + (n_dp - 1))
 
     def up(kind, hop, i):
@@ -153,6 +154,9 @@
             ).wait_recv()
 
         each(a, b, one)
+
+    loads[2].wait()
+    loads[3].wait()
 
     stage[...] = q_raw[...].astype(jnp.float32).reshape(rows * q_heads, width)
     scale = score_scale * math.log2(math.e)
@@ -194,17 +198,31 @@
 
         lax.fori_loop(0, heads, head, 0)
 
-    def mix(d, a, b):
+    def mix(blocks, a, b, fresh=False, last=False):
         count = b - a
-        stage[0 : count * heads, :] = raw[1, d, a:b].astype(jnp.float32).reshape(count * heads, width)
-
-        def head(h, _):
-            v = stage[pl.ds(h, count, stride=heads), :].astype(jnp.bfloat16)
-            o = jnp.dot(weights[d, h, :, a:b], v, preferred_element_type=jnp.float32)
-            acc[h] = acc[h] + peaks[h, :, d : d + 1] * o
+        for j, d in enumerate(blocks):
+            stage[j * count * heads : (j + 1) * count * heads, :] = (
+                raw[1, d, a:b].astype(jnp.float32).reshape(count * heads, width)
+            )
+
+        def head(h):
+            o = None if fresh else acc[h]
+            for j, d in enumerate(blocks):
+                v = stage[pl.ds(j * count * heads + h, count, stride=heads), :].astype(jnp.bfloat16)
+                more = jnp.dot(weights[d, h, :, a:b], v, preferred_element_type=jnp.float32)
+                o = more if o is None else o + more
+            if last:
+                for g in range(group):
+                    spread[pl.ds(h * group + g, rows, stride=q_heads), :] = o[g * rows : (g + 1) * rows]
+            else:
+                acc[h] = o
+
+        def pair(i, _):
+            for j in range(UNROLL):
+                head(i * UNROLL + j)
             return 0
 
-        lax.fori_loop(0, heads, head, 0)
+        lax.fori_loop(0, heads // UNROLL, pair, 0)
 
     score(0)
 
@@ -241,7 +259,9 @@
         peak = jnp.max(m, axis=1, keepdims=True)
         a = jnp.exp2(m - peak)
         total = jnp.sum(a * totals[h], axis=1, keepdims=True)
-        peaks[h] = a / total
+        share = a / total
+        for d in range(reach + 1):
+            weights[d, h] = (weights[d, h].astype(jnp.float32) * share[:, d : d + 1]).astype(jnp.bfloat16)
         lse = peak * math.log(2.0) + jnp.log(total)
         return square + jnp.sum(lse * lse, axis=0, keepdims=True)
 
@@ -249,7 +269,18 @@
     mine[...] = jnp.broadcast_to(square, mine.shape)
     parts_seq[me] = jnp.broadcast_to(square, mine.shape)
 
-    mix(0, 0, rows)
+    @pl.when(chip >= 1)
+    def _():
+        take(1, 1, 1, 2)
+
+    @pl.when(first)
+    def _():
+        mix((0,), 0, rows, fresh=True)
+
+    @pl.when(second)
+    def _():
+        take_across(1, 0, 0, CHUNKS)
+        mix((0, 1), 0, rows, fresh=True)
 
     def tell_seq(j):
         return pltpu.make_async_remote_copy(
@@ -277,25 +308,11 @@
 
     each(1, n, lambda j: tell_seq(j).start())
 
-    @pl.when(second)
-    def _():
-        take_across(1, 0, 0, CHUNKS)
-        mix(1, 0, rows)
-
     @pl.when(chip >= 1)
     def _():
-        take(1, 1, 1, CHUNKS)
-        mix(2, 0, rows)
-
-        @pl.when(first)
-        def _():
-            take_across(1, 0, 0, CHUNKS)
-            mix(1, 0, rows)
-
-        @pl.when(second)
-        def _():
-            take_across(1, 1, 0, CHUNKS)
-            mix(3, 0, rows)
+        take(1, 1, 2, CHUNKS)
+        take_across(1, core, 0, CHUNKS)
+        mix((2, 1 + 2 * core), 0, rows)
 
     each(1, n, lambda j: heard_seq(j).wait_recv())
     column = jnp.sum(parts_seq[...], axis=0)
@@ -307,12 +324,15 @@
     @pl.when(chip >= 2)
     def _():
         take(1, 2, 0, CHUNKS // 2)
-        mix(4, 0, middle)
+
+        @pl.when(second)
+        def _():
+            mix((4,), 0, middle)
 
         @pl.when(first)
         def _():
             take_across(1, 1, 0, CHUNKS // 2)
-            mix(3, 0, middle)
+            mix((4, 3), 0, middle)
 
     each(1, n_dp, lambda j: tell_dp(j).start())
     each(1, n_dp, lambda j: heard_dp(j).wait_recv())
@@ -321,20 +341,26 @@
     @pl.when(chip >= 2)
     def _():
         take(1, 2, CHUNKS // 2, CHUNKS)
-        mix(4, middle, rows)
+
+        @pl.when(second)
+        def _():
+            mix((4,), middle, rows, last=True)
 
         @pl.when(first)
         def _():
             take_across(1, 1, CHUNKS // 2, CHUNKS)
-            mix(3, middle, rows)
+            mix((4, 3), middle, rows, last=True)
 
     def give(h, _):
         for g in range(group):
-            stage[pl.ds(h * group + g, rows, stride=q_heads), :] = acc[h, g * rows : (g + 1) * rows, :]
+            spread[pl.ds(h * group + g, rows, stride=q_heads), :] = acc[h, g * rows : (g + 1) * rows, :]
         return 0
 
-    lax.fori_loop(0, heads, give, 0)
-    out[...] = stage[...].reshape(rows, q_heads, width).astype(jnp.bfloat16)
+    @pl.when(chip < 2)
+    def _():
+        lax.fori_loop(0, heads, give, 0)
+
+    out[...] = spread[...].reshape(rows, q_heads, width).astype(jnp.bfloat16)
 
     def sent_up(kind, hop):
         each(0, CHUNKS, lambda i: up(kind, hop, i).wait_send())
@@ -372,11 +398,13 @@
             jax.ShapeDtypeStruct((rows, q_heads, width), jnp.bfloat16),
             jax.ShapeDtypeStruct((1, 1), jnp.float32),
         ),
-        in_specs=[smem, anywhere, anywhere, anywhere, vmem],
+        in_specs=[smem, anywhere, anywhere, anywhere, anywhere],
         out_specs=(vmem, smem),
         scratch_shapes=[
+            pltpu.VMEM(tab.shape, jnp.float32),
             pltpu.VMEM((rows, q_heads, width), jnp.bfloat16),
             pltpu.VMEM((2, reach + 1, rows, heads, width), jnp.bfloat16),
+            pltpu.VMEM((rows * q_heads, width), jnp.float32),
             pltpu.VMEM((rows * q_heads, width), jnp.float32),
             pltpu.VMEM((heads, group * rows, width), jnp.bfloat16),
             pltpu.VMEM((reach + 1, heads, group * rows, rows), jnp.bfloat16),
@@ -389,7 +417,7 @@
             pltpu.VMEM((n, 8, width), jnp.float32),
             pltpu.VMEM((8, width), jnp.float32),
             pltpu.VMEM((n_dp, 8, width), jnp.float32),
-            dma((3,)),
+            dma((4,)),
             dma((2, hops, CHUNKS)),
             dma((2, hops, CHUNKS)),
             dma((2, hops, CHUNKS)),

time: 66.5 us -> 64 us (0.962)
  Pallas kernels: 61.6 us -> 59.1 us
    pallas_call x1, Pallas kernels: 61.6 us -> 59.1 us  [shards(): pl.pallas_call(functools.partial(body, n, n_dp, reach), out_shape=(jax.Sh...]
where the time goes in v2:
time: 64 us; the launch traced here: 63.8 us
  Pallas kernels  59.1 us (92%)
  local copies, waits for them, and re-layouts  2.37 us (4%)
  between operations  2.33 us (4%)
    pallas_call x1, Pallas kernels, shards(): pl.pallas_call(functools.partial(body, n, n_dp, reach), out_shape=(jax.Sh...  59.1 us
    unnamed x1, local copies, waits for them, and re-layouts  2.37 us

profile of v2, /device:TPU:16, one launch (start us, length us, event | category | flops | bytes accessed | tf_op | source)
XLA Modules:
  0.0 63.8 jit_solution(16008174367846343415)
XLA Ops:
  0.6 59.1 %attend.1 = (bf16[256,16,128]{2,1,0:T(8,128)(2,1)}, f32[1,1]{1,0:T(1,128)}) custom-call(s32[1,8]{1,0:T(1,128)} %lengths.1, bf16[256,16,128]{2,1,0:T(8,128)(2,1)} %bitcast.5, bf16[256,8,128]{2,1,0:T(8,128)(2,1)} %bitcast.7, bf16[256,8,128]{2,1,0:T(8,128)(2,1)} %bitcast.8, f32[5,2,256,128]{3,2,1,0:T(8,128)} %constant.2.clone.tab_hbm), custom_call_target="tpu_custom_call" | custom-call | tf_op jit(solution)/shard_map/attend/pallas_call | solution.py:395
  59.7 2.4 %copy.9 = bf16[1,256,16,128]{3,2,1,0:T(8,128)(2,1)} copy(bf16[1,256,16,128]{3,2,1,0:T(8,128)(2,1)} %bitcast.6) | data formatting | bytes 2097152

commit v3 on v2

--- a/solution.py
+++ b/solution.py
@@ -15,7 +15,7 @@
 masked = -1e30
 MESH = pl.DeviceIdType.MESH
 CHUNKS = 4
-UNROLL = 2
+UNROLL = 8
 
 
 def tables(rows, reach, width):
@@ -206,11 +206,14 @@
             )
 
         def head(h):
-            o = None if fresh else acc[h]
-            for j, d in enumerate(blocks):
-                v = stage[pl.ds(j * count * heads + h, count, stride=heads), :].astype(jnp.bfloat16)
-                more = jnp.dot(weights[d, h, :, a:b], v, preferred_element_type=jnp.float32)
-                o = more if o is None else o + more
+            v = [
+                stage[pl.ds(j * count * heads + h, count, stride=heads), :].astype(jnp.bfloat16)
+                for j in range(len(blocks))
+            ]
+            w = [weights[d, h, :, a:b] for d in blocks]
+            o = jnp.dot(jnp.concatenate(w, axis=1), jnp.concatenate(v, axis=0), preferred_element_type=jnp.float32)
+            if not fresh:
+                o = acc[h] + o
             if last:
                 for g in range(group):
                     spread[pl.ds(h * group + g, rows, stride=q_heads), :] = o[g * rows : (g + 1) * rows]
@@ -259,9 +262,7 @@
         peak = jnp.max(m, axis=1, keepdims=True)
         a = jnp.exp2(m - peak)
         total = jnp.sum(a * totals[h], axis=1, keepdims=True)
-        share = a / total
-        for d in range(reach + 1):
-            weights[d, h] = (weights[d, h].astype(jnp.float32) * share[:, d : d + 1]).astype(jnp.bfloat16)
+        peaks[h] = a / total
         lse = peak * math.log(2.0) + jnp.log(total)
         return square + jnp.sum(lse * lse, axis=0, keepdims=True)
 
@@ -269,9 +270,46 @@
     mine[...] = jnp.broadcast_to(square, mine.shape)
     parts_seq[me] = jnp.broadcast_to(square, mine.shape)
 
+    def tell_seq(j):
+        return pltpu.make_async_remote_copy(
+            src_ref=mine, dst_ref=parts_seq.at[me], send_sem=s_send.at[j], recv_sem=s_recv.at[j],
+            device_id={"seq": lax.rem(me + j, n)}, device_id_type=MESH,
+        )
+
+    def heard_seq(j):
+        return pltpu.make_async_remote_copy(
+            src_ref=mine, dst_ref=parts_seq.at[lax.rem(me + n - j, n)], send_sem=s_send.at[j], recv_sem=s_recv.at[j],
+            device_id={"seq": lax.rem(me + j, n)}, device_id_type=MESH,
+        )
+
+    def tell_dp(j):
+        return pltpu.make_async_remote_copy(
+            src_ref=mine2, dst_ref=parts_dp.at[dp], send_sem=p_send.at[j], recv_sem=p_recv.at[j],
+            device_id={"dp": lax.rem(dp + j, n_dp)}, device_id_type=MESH,
+        )
+
+    def heard_dp(j):
+        return pltpu.make_async_remote_copy(
+            src_ref=mine2, dst_ref=parts_dp.at[lax.rem(dp + n_dp - j, n_dp)], send_sem=p_send.at[j], recv_sem=p_recv.at[j],
+            device_id={"dp": lax.rem(dp + j, n_dp)}, device_id_type=MESH,
+        )
+
     @pl.when(chip >= 1)
     def _():
         take(1, 1, 1, 2)
+
+    each(1, n, lambda j: tell_seq(j).start())
+
+    def portion(h, _):
+        for d in range(reach + 1):
+            weights[d, h] = (weights[d, h].astype(jnp.float32) * peaks[h, :, d : d + 1]).astype(jnp.bfloat16)
+        return 0
+
+    lax.fori_loop(0, heads, portion, 0)
+
+    @pl.when(chip >= 1)
+    def _():
+        take(1, 1, 2, CHUNKS)
 
     @pl.when(first)
     def _():
@@ -282,35 +320,8 @@
         take_across(1, 0, 0, CHUNKS)
         mix((0, 1), 0, rows, fresh=True)
 
-    def tell_seq(j):
-        return pltpu.make_async_remote_copy(
-            src_ref=mine, dst_ref=parts_seq.at[me], send_sem=s_send.at[j], recv_sem=s_recv.at[j],
-            device_id={"seq": lax.rem(me + j, n)}, device_id_type=MESH,
-        )
-
-    def heard_seq(j):
-        return pltpu.make_async_remote_copy(
-            src_ref=mine, dst_ref=parts_seq.at[lax.rem(me + n - j, n)], send_sem=s_send.at[j], recv_sem=s_recv.at[j],
-            device_id={"seq": lax.rem(me + j, n)}, device_id_type=MESH,
-        )
-
-    def tell_dp(j):
-        return pltpu.make_async_remote_copy(
-            src_ref=mine2, dst_ref=parts_dp.at[dp], send_sem=p_send.at[j], recv_sem=p_recv.at[j],
-            device_id={"dp": lax.rem(dp + j, n_dp)}, device_id_type=MESH,
-        )
-
-    def heard_dp(j):
-        return pltpu.make_async_remote_copy(
-            src_ref=mine2, dst_ref=parts_dp.at[lax.rem(dp + n_dp - j, n_dp)], send_sem=p_send.at[j], recv_sem=p_recv.at[j],
-            device_id={"dp": lax.rem(dp + j, n_dp)}, device_id_type=MESH,
-        )
-
-    each(1, n, lambda j: tell_seq(j).start())
-
     @pl.when(chip >= 1)
     def _():
-        take(1, 1, 2, CHUNKS)
         take_across(1, core, 0, CHUNKS)
         mix((2, 1 + 2 * core), 0, rows)
 
@@ -335,8 +346,6 @@
             mix((4, 3), 0, middle)
 
     each(1, n_dp, lambda j: tell_dp(j).start())
-    each(1, n_dp, lambda j: heard_dp(j).wait_recv())
-    z_out[0, 0] = jnp.sum(jnp.sum(parts_dp[...], axis=0)[0:1, 0:1]) / (n_dp * n * rows * q_heads)
 
     @pl.when(chip >= 2)
     def _():
@@ -361,6 +370,9 @@
         lax.fori_loop(0, heads, give, 0)
 
     out[...] = spread[...].reshape(rows, q_heads, width).astype(jnp.bfloat16)
+
+    each(1, n_dp, lambda j: heard_dp(j).wait_recv())
+    z_out[0, 0] = jnp.sum(jnp.sum(parts_dp[...], axis=0)[0:1, 0:1]) / (n_dp * n * rows * q_heads)
 
     def sent_up(kind, hop):
         each(0, CHUNKS, lambda i: up(kind, hop, i).wait_send())

time: 64 us -> 60.3 us (0.942)
  Pallas kernels: 59.1 us -> 55.4 us
    pallas_call x1, Pallas kernels: 59.1 us -> 55.4 us  [shards(): pl.pallas_call(functools.partial(body, n, n_dp, reach), out_shape=(jax.Sh...]
where the time goes in v3:
time: 60.3 us; the launch traced here: 60.1 us
  Pallas kernels  55.4 us (92%)
  local copies, waits for them, and re-layouts  2.37 us (4%)
  between operations  2.33 us (4%)
    pallas_call x1, Pallas kernels, shards(): pl.pallas_call(functools.partial(body, n, n_dp, reach), out_shape=(jax.Sh...  55.4 us
    unnamed x1, local copies, waits for them, and re-layouts  2.37 us

profile of v3, /device:TPU:16, one launch (start us, length us, event | category | flops | bytes accessed | tf_op | source)
XLA Modules:
  0.0 60.1 jit_solution(2077668333401536177)
XLA Ops:
  0.6 55.4 %attend.1 = (bf16[256,16,128]{2,1,0:T(8,128)(2,1)}, f32[1,1]{1,0:T(1,128)}) custom-call(s32[1,8]{1,0:T(1,128)} %lengths.1, bf16[256,16,128]{2,1,0:T(8,128)(2,1)} %bitcast.5, bf16[256,8,128]{2,1,0:T(8,128)(2,1)} %bitcast.7, bf16[256,8,128]{2,1,0:T(8,128)(2,1)} %bitcast.8, f32[5,2,256,128]{3,2,1,0:T(8,128)} %constant.2.clone.tab_hbm), custom_call_target="tpu_custom_call" | custom-call | tf_op jit(solution)/shard_map/attend/pallas_call | solution.py:407
  56.0 2.4 %copy.9 = bf16[1,256,16,128]{3,2,1,0:T(8,128)(2,1)} copy(bf16[1,256,16,128]{3,2,1,0:T(8,128)(2,1)} %bitcast.6) | data formatting | bytes 2097152
